TPU v7x, 32 devices: a whole 2x2x4 slice. The times are simulated.
32 devices in a mesh: band: 16 (over z, y, x), ga: 2 (over core).
Axes of the slice: x: 2, y: 2, z: 4, core: 2. Of those that a mesh axis runs over, the one named last changes fastest.
Arguments:
- matrix_elements: float32 [2, 4096, 12288], P(None, 'band', 'ga'), may hold values from -6 to 6
- band_index: int32 [4096], P('band'), may hold values from 0 to 1048575
- occupied: int32 [1], replicated, may hold values from 262144 to 786432
- band_weight: float32 [4096], P('band'), may hold values from 0.3 to 3
- coulomb: float32 [12288], replicated, may hold values from 0.2 to 5
Outputs:
- sigma: float32 [12288, 2, 512], P(('ga', 'band'))
All inputs are finite; a program needn't handle non-finite values.
Results may differ from a plain program's by a relative error of at most 0.00018.
Values sent between devices are 32-bit elements; how exact they have to be, the bound alone decides.
A program may use at most 192 MiB of HBM per device.

v0:
```python
import math
import jax
import jax.numpy as jnp
from jax import lax
from jax.sharding import PartitionSpec as P

COLS = 512


def spread(x, axis, root):
    mine = lax.axis_index(axis) == root
    return lax.psum(jnp.where(mine, x, jnp.zeros_like(x)), axis)


def contract(left, right):
    return lax.dot_general(
        left,
        right,
        (((0,), (0,)), ((), ())),
        precision=lax.Precision.HIGHEST,
        preferred_element_type=jnp.float32,
    )


def right_side(slab):
    return jnp.concatenate(
        [jnp.concatenate([slab[0], slab[1]], 1), jnp.concatenate([slab[1], -slab[0]], 1)], 0
    )


def defects(coef, block):
    square = 2.0 - block[0] * block[0] - block[1] * block[1]
    return jnp.dot(
        coef, square, precision=lax.Precision.HIGHEST, preferred_element_type=jnp.float32
    )


def body(matrix_elements, band_index, occupied, band_weight, coulomb):
    bands_dev = matrix_elements.shape[1]
    half = matrix_elements.shape[2]
    n_band = lax.axis_size("band")
    rows_dev = half // n_band
    factor = 1.0 / math.sqrt(bands_dev * n_band)
    occ = (band_index < occupied[0]).astype(jnp.float32)
    coef = (0.5 - occ) * band_weight
    slab = spread(matrix_elements[:, :, :COLS], "ga", 0)
    band_pos = lax.axis_index("band")
    ga_pos = lax.axis_index("ga")
    left = jnp.concatenate(
        [coef[:, None] * matrix_elements[0], coef[:, None] * matrix_elements[1]], 0
    )
    right = right_side(slab)
    sums = lax.psum_scatter(contract(left, right), "band", scatter_dimension=0, tiled=True)
    defect_full = defects(coef, matrix_elements)
    defect_slab = defects(coef, slab)
    row_def = lax.psum_scatter(defect_full, "band", scatter_dimension=0, tiled=True)
    col_def = lax.psum(defect_slab, "band")
    sums = sums * factor
    row_def = row_def * factor
    col_def = col_def * factor
    row_coul = lax.dynamic_slice_in_dim(coulomb, ga_pos * half + band_pos * rows_dev, rows_dev, 0)
    weight = jnp.sqrt(row_coul[:, None] * coulomb[None, :COLS])
    part_re = weight * (sums[:, :COLS] + 0.5 * (row_def[:, None] + col_def[None, :]))
    part_im = weight * sums[:, COLS:]
    return jnp.stack([part_re, part_im], 1)


def solution(mesh):
    return jax.shard_map(
        body,
        mesh=mesh,
        in_specs=(P(None, "band", "ga"), P("band"), P(), P("band"), P()),
        out_specs=P(("ga", "band"), None, None),
        check_vma=False,
    )
```

profile of v0, /device:TPU:0, one launch (start us, length us, event | category | flops | bytes accessed | tf_op | source)
XLA Modules:
  0.0 451.3 jit_solution(16196607224541450727)
XLA Ops:
  6.5 2.3 slice_select_fusion
  8.8 0.0 all-reduce.4.cloned.1.call-update
  8.8 0.0 reduce-scatter.2.cloned.1.call-start
  9.5 0.7 fusion.29
  10.2 11.4 %bitcast_multiply_fusion.3 = (f32[256,6144]{1,0:T(8,128)}, f32[256,6144]{1,0:T(8,128)}) fusion(f32[2,256,6144]{2,1,0:T(8,128)} %param.5, f32[256]{0:T(256)S(1)} %fusion.29), kind=kLoop, calls=%fused_computation.9 | loop fusion | flops 3145728 | bytes 25166848 | tf_op jit(solution)/shard_map/mul | solution.py:50
  21.6 10.2 %all-reduce.4.cloned.1.call-done = f32[2,256,512]{2,1,0:T(8,128)} async-done(((f32[2,256,512]{2,1,0:T(8,128)}), f32[2,256,512]{2,1,0:T(8,128)}) %all-reduce.4.cloned.1.call-update) | async-done | bytes 1048592 | tf_op jit(solution)/shard_map/psum | solution.py:12
  31.8 1.1 fusion.33
  32.9 1.3 slice_bitcast_fusion.1
  34.2 44.8 %fusion = f32[6144,1024]{1,0:T(8,128)} fusion(f32[256,6144]{1,0:T(8,128)} %get-tuple-element.8, f32[256,6144]{1,0:T(8,128)} %get-tuple-element.7, f32[256,512]{1,0:T(8,128)S(1)} %fusion.33, f32[256,512]{1,0:T(8,128)S(1)} %get-tuple-element.12, f32[256,512]{1,0:T(8,128)S(1)} %get-tuple-element.11), kind=kOutput, calls=%fused_computation | convolution fusion | flops 38659424256 | bytes 39321600 | tf_op jit(solution)/shard_map/dot_general | solution.py:16
  79.0 0.0 reduce-scatter.2.cloned.1.call-update
  79.0 0.7 copy-done.1
  79.8 0.1 dynamic_slice.3
  79.8 0.0 copy-done.2
  79.8 0.6 dynamic-slice
  81.1 0.0 slice-start
  81.1 8.5 %fusion.5 = f32[1,6144]{1,0:T(1,128)S(1)} fusion(f32[256,1]{0,1:T(1,128)S(1)} %bitcast.40, f32[2,256,6144]{2,1,0:T(8,128)} %param.5), kind=kOutput, calls=%fused_computation.7 | convolution fusion | flops 25165824 | bytes 12608512 | tf_op jit(solution)/shard_map/dot_general | solution.py:33
  89.5 0.4 fusion.22
  90.0 82.0 %all-reduce.1 = (f32[512]{0:T(512)S(1)}, f32[6144]{0:T(1024)S(1)}) all-reduce(f32[512]{0:T(512)S(1)} %bitcast.42, f32[6144]{0:T(1024)S(1)} %bitcast.39), channel_id=1, replica_groups=mesh['band'=16,'ga'=2] {'band'}, use_global_device_ids=true, to_apply=%region_3.4 | all-reduce | flops 6656 | bytes 53248 | tf_op jit(solution)/shard_map/psum | solution.py:57
  172.0 0.1 dynamic-slice_multiply_fusion
  172.0 267.9 %reduce-scatter.2.cloned.1.call-done = f32[384,1024]{1,0:T(8,128)} async-done(((f32[6144,1024]{1,0:T(8,128)}), f32[384,1024]{1,0:T(8,128)}) %reduce-scatter.2.cloned.1.call-update) | async-done | bytes 1572880 | tf_op jit(solution)/shard_map/reduce_scatter | solution.py:53
  439.9 1.6 broadcast_multiply_fusion
  441.5 0.4 fusion.21
  441.9 0.1 pad_maximum_fusion
  442.1 2.4 copy.7
  (7 shorter events, 0.0 us)
Async XLA Ops:
  6.5 25.3 %all-reduce.4.cloned.1.call-start = ((), (), s32[]{:S(2)}) async-start(), calls=%async_computation.1 | async-start | bytes 2097152 | tf_op jit(solution)/shard_map/psum | solution.py:12
  8.8 431.1 %reduce-scatter.2.cloned.1.call-start = ((), (), s32[]{:S(2)}) async-start(), calls=%async_computation.2 | async-start | bytes 26738688 | tf_op jit(solution)/shard_map/reduce_scatter | solution.py:53
  79.0 0.8 copy-start.1
  79.0 0.9 copy-start.2
  79.0 10.6 %copy-start = (f32[2,256,512]{2,1,0:T(8,128)S(1)}, f32[2,256,512]{2,1,0:T(8,128)}, u32[]{:S(2)}) copy-start(f32[2,256,512]{2,1,0:T(8,128)} %all-reduce.4.cloned.1.call-done) | copy-start | bytes 3145732
  81.1 360.4 %slice-start = ((f32[12288]{0:T(1024)}), f32[512]{0:T(512)S(1)}, s32[]{:S(2)}) async-start(f32[12288]{0:T(1024)} %param.9), calls=%async_computation.3 | async-start | bytes 4096 | tf_op jit(solution)/shard_map/slice | solution.py:62
Sparse Core Ops, SparseCore 0:
  9.7 22.1 all-reduce.3
  79.1 360.7 reduce-scatter.1
where the time goes:
time: 452 us; the launch traced here: 451 us
  waiting for transfers between devices  278 us (62%)
  blocking collectives  82 us (18%)
  matrix products  53.6 us (12%)
  other arithmetic  17.7 us (4%)
  between operations  14.8 us (3%)
  local copies, waits for them, and re-layouts  5.05 us (1%)
    reduce_scatter x1, waiting for transfers between devices, body(): lax.psum_scatter(contract(left, right), 'band', scatter_dimension=0, tile...  268 us
    psum x1, blocking collectives, body(): col_def = lax.psum(defect_slab, 'band')  82 us
    dot_general x1, matrix products, contract(): lax.dot_general(left, right, (((0,), (0,)), ((), ())), precision=lax.Prec...  44.8 us
    mul x1, other arithmetic, body(): coef[:, None] * matrix_elements[0]  11.4 us
    psum x1, waiting for transfers between devices, spread(): return lax.psum(jnp.where(mine, x, jnp.zeros_like(x)), axis)  10.2 us
  transfers between devices with their start and end apart: 2, of which 2 were waited for; matrix products, arithmetic and copies ran while one was open for 5% of the time, Pallas kernels for 0%

commit v1 on v0

--- a/solution.py
+++ b/solution.py
@@ -54,7 +54,7 @@
     defect_full = defects(coef, matrix_elements)
     defect_slab = defects(coef, slab)
     row_def = lax.psum_scatter(defect_full, "band", scatter_dimension=0, tiled=True)
-    col_def = lax.psum(defect_slab, "band")
+    col_def = jnp.sum(lax.all_gather(defect_slab, "band"), axis=0)
     sums = sums * factor
     row_def = row_def * factor
     col_def = col_def * factor

time: 452 us -> 453 us (level)
  blocking collectives: 82 us -> 119 us
  waiting for transfers between devices: 278 us -> 242 us
    psum x1 -> x0, blocking collectives: 82 us -> none  [body(): col_def = lax.psum(defect_slab, 'band')]
    unnamed x0 -> x1, blocking collectives: none -> 81.8 us
    all_gather x0 -> x1, blocking collectives: none -> 37.6 us  [body(): col_def = jnp.sum(lax.all_gather(defect_slab, 'band'), axis=0)]
    reduce_scatter x1, waiting for transfers between devices: 268 us -> 232 us  [body(): lax.psum_scatter(contract(left, right), 'band', scatter_dimension=0, tile...]
where the time goes in v1:
time: 453 us; the launch traced here: 452 us
  waiting for transfers between devices  242 us (53%)
  blocking collectives  119 us (26%)
  matrix products  53.6 us (12%)
  other arithmetic  17.7 us (4%)
  between operations  14.8 us (3%)
  local copies, waits for them, and re-layouts  5.05 us (1%)
    reduce_scatter x1, waiting for transfers between devices, body(): lax.psum_scatter(contract(left, right), 'band', scatter_dimension=0, tile...  232 us
    unnamed x1, blocking collectives  81.8 us
    dot_general x1, matrix products, contract(): lax.dot_general(left, right, (((0,), (0,)), ((), ())), precision=lax.Prec...  44.8 us
    all_gather x1, blocking collectives, body(): col_def = jnp.sum(lax.all_gather(defect_slab, 'band'), axis=0)  37.6 us
    mul x1, other arithmetic, body(): coef[:, None] * matrix_elements[0]  11.4 us
    psum x1, waiting for transfers between devices, spread(): return lax.psum(jnp.where(mine, x, jnp.zeros_like(x)), axis)  10.2 us
  transfers between devices with their start and end apart: 2, of which 2 were waited for; matrix products, arithmetic and copies ran while one was open for 5% of the time, Pallas kernels for 0%

profile of v1, /device:TPU:0, one launch (start us, length us, event | category | flops | bytes accessed | tf_op | source)
XLA Modules:
  0.0 452.4 jit_solution(7595040104415083493)
XLA Ops:
  6.5 2.3 slice_select_fusion
  8.8 0.0 all-reduce.3.cloned.1.call-update
  8.8 0.0 reduce-scatter.2.cloned.1.call-start
  9.5 0.7 fusion.28
  10.2 11.4 %bitcast_multiply_fusion.3 = (f32[256,6144]{1,0:T(8,128)}, f32[256,6144]{1,0:T(8,128)}) fusion(f32[2,256,6144]{2,1,0:T(8,128)} %param.5, f32[256]{0:T(256)S(1)} %fusion.28), kind=kLoop, calls=%fused_computation.9 | loop fusion | flops 3145728 | bytes 25166848 | tf_op jit(solution)/shard_map/mul | solution.py:50
  21.7 10.2 %all-reduce.3.cloned.1.call-done = f32[2,256,512]{2,1,0:T(8,128)} async-done(((f32[2,256,512]{2,1,0:T(8,128)}), f32[2,256,512]{2,1,0:T(8,128)}) %all-reduce.3.cloned.1.call-update) | async-done | bytes 1048592 | tf_op jit(solution)/shard_map/psum | solution.py:12
  31.8 1.1 fusion.32
  32.9 1.3 slice_bitcast_fusion.1
  34.2 44.8 %fusion = f32[6144,1024]{1,0:T(8,128)} fusion(f32[256,6144]{1,0:T(8,128)} %get-tuple-element.6, f32[256,6144]{1,0:T(8,128)} %get-tuple-element.5, f32[256,512]{1,0:T(8,128)S(1)} %fusion.32, f32[256,512]{1,0:T(8,128)S(1)} %get-tuple-element.10, f32[256,512]{1,0:T(8,128)S(1)} %get-tuple-element.9), kind=kOutput, calls=%fused_computation | convolution fusion | flops 38659424256 | bytes 39321600 | tf_op jit(solution)/shard_map/dot_general | solution.py:16
  79.0 0.0 reduce-scatter.2.cloned.1.call-update
  79.0 0.7 copy-done.1
  79.8 0.1 dynamic_slice.3
  79.8 0.6 dynamic-slice
  81.1 0.0 slice-start
  81.1 8.5 %fusion.5 = f32[1,6144]{1,0:T(1,128)S(1)} fusion(f32[256,1]{0,1:T(1,128)S(1)} %bitcast.43, f32[2,256,6144]{2,1,0:T(8,128)} %param.5), kind=kOutput, calls=%fused_computation.7 | convolution fusion | flops 25165824 | bytes 12608512 | tf_op jit(solution)/shard_map/dot_general | solution.py:33
  89.5 81.8 %all-reduce = f32[6144]{0:T(1024)S(1)} all-reduce(f32[6144]{0:T(1024)S(1)} %bitcast.42), channel_id=4, replica_groups=mesh['band'=16,'ga'=2] {'band'}, use_global_device_ids=true, to_apply=%region_2.3.clone | all-reduce | flops 6144 | bytes 49152
  171.3 0.1 dynamic-slice_multiply_fusion
  171.4 0.4 convolution_bitcast_fusion
  171.8 37.6 %all-gather.1 = f32[16,1,512]{2,1,0:T(1,128)S(1)} all-gather(f32[1,1,512]{2,1,0:T(1,128)S(1)} %convolution_bitcast_fusion), channel_id=2, replica_groups=mesh['band'=16,'ga'=2] {'band'}, dimensions={0}, use_global_device_ids=true | all-gather | bytes 34816 | tf_op jit(solution)/shard_map/all_gather | solution.py:57
  209.5 231.6 %reduce-scatter.2.cloned.1.call-done = f32[384,1024]{1,0:T(8,128)} async-done(((f32[6144,1024]{1,0:T(8,128)}), f32[384,1024]{1,0:T(8,128)}) %reduce-scatter.2.cloned.1.call-update) | async-done | bytes 1572880 | tf_op jit(solution)/shard_map/reduce_scatter | solution.py:53
  441.1 1.6 broadcast_multiply_fusion
  442.7 0.4 fusion.21
  443.1 0.1 pad_maximum_fusion
  443.2 2.4 copy.7
  (9 shorter events, 0.1 us)
Async XLA Ops:
  6.5 25.3 %all-reduce.3.cloned.1.call-start = ((), (), s32[]{:S(2)}) async-start(), calls=%async_computation.1 | async-start | bytes 2097152 | tf_op jit(solution)/shard_map/psum | solution.py:12
  8.8 432.2 %reduce-scatter.2.cloned.1.call-start = ((), (), s32[]{:S(2)}) async-start(), calls=%async_computation.2 | async-start | bytes 26738688 | tf_op jit(solution)/shard_map/reduce_scatter | solution.py:53
  79.0 0.8 copy-start.1
  79.0 0.9 copy-start.2
  79.0 92.4 %copy-start = (f32[2,256,512]{2,1,0:T(8,128)S(1)}, f32[2,256,512]{2,1,0:T(8,128)}, u32[]{:S(2)}) copy-start(f32[2,256,512]{2,1,0:T(8,128)} %all-reduce.3.cloned.1.call-done) | copy-start | bytes 3145732
  81.1 361.6 %slice-start = ((f32[12288]{0:T(1024)}), f32[512]{0:T(512)S(1)}, s32[]{:S(2)}) async-start(f32[12288]{0:T(1024)} %param.9), calls=%async_computation.3 | async-start | bytes 4096 | tf_op jit(solution)/shard_map/slice | solution.py:62
Sparse Core Ops, SparseCore 0:
  9.7 22.1 all-reduce.2
  79.1 361.9 reduce-scatter.1
